TPU v7x, 32 devices: a whole 2x2x4 slice. The times are simulated.
32 devices in a mesh: replica: 4 (over y, x), fsdp: 8 (over z, core).
Axes of the slice: x: 2, y: 2, z: 4, core: 2. Of those that a mesh axis runs over, the one named last changes fastest.
Arguments:
- codes: int32 [4, 8192, 4096], P('replica', None, 'fsdp'), may hold values from -127 to 127
- scales: float32 [4, 32, 8192], P('replica', 'fsdp'), may hold values from 0.002 to 0.03
- master: float32 [8192, 4096], P(('replica', 'fsdp')), may hold values from -6 to 6
- momentum: float32 [8192, 4096], P(('replica', 'fsdp')), may hold values from -6 to 6
Outputs:
- new_master: float32 [8192, 4096], P(('replica', 'fsdp'))
- new_momentum: float32 [8192, 4096], P(('replica', 'fsdp'))
- weights: bfloat16 [8192, 4096], P(None, 'fsdp')
All inputs are finite; a program needn't handle non-finite values.
Results may differ from a plain program's by a relative error of at most 0.0075.
Values may be sent and summed in bfloat16 or wider, within the bound.
A program may use at most 128 MiB of HBM per device.

v0:
```python
import jax
import jax.numpy as jnp
from jax import lax
from jax.sharding import PartitionSpec as P

outer_rate = 0.7
momentum_factor = 0.9


def dequantize(codes, scales):
    block_count = scales.shape[1]
    total_rows = codes.shape[1]
    width = codes.shape[2]
    scaled = codes[0].astype(jnp.float32).reshape(total_rows, block_count, width // block_count)
    return (scaled * jnp.transpose(scales[0])[:, :, None]).reshape(total_rows, width)


def outer_update(summed, master, momentum, replica_count):
    mean_delta = summed / replica_count
    new_momentum = momentum_factor * momentum + mean_delta
    new_master = master - outer_rate * (mean_delta + momentum_factor * new_momentum)
    return (new_master, new_momentum)


def local(codes, scales, master, momentum):
    replica_count = lax.axis_size("replica")
    delta_local = dequantize(codes, scales)
    partial_sum = lax.psum_scatter(
        delta_local.astype(jnp.bfloat16), "replica", scatter_dimension=0, tiled=True
    ).astype(jnp.float32)
    summed = lax.all_to_all(
        partial_sum.astype(jnp.bfloat16), "fsdp", split_axis=0, concat_axis=1, tiled=True
    ).astype(partial_sum.dtype)
    new_master, new_momentum = outer_update(summed, master, momentum, replica_count)
    rounded = new_master.astype(jnp.bfloat16)
    columns = lax.all_to_all(rounded, "fsdp", split_axis=1, concat_axis=0, tiled=True)
    weights = lax.all_gather(columns, "replica", axis=0, tiled=True)
    return (new_master, new_momentum, weights)


def solution(mesh):
    return jax.shard_map(
        local,
        mesh=mesh,
        in_specs=(
            P("replica", None, "fsdp"),
            P("replica", "fsdp", None),
            P(("replica", "fsdp"), None),
            P(("replica", "fsdp"), None),
        ),
        out_specs=(P(("replica", "fsdp"), None), P(("replica", "fsdp"), None), P(None, "fsdp")),
        check_vma=False,
    )
```

profile of v0, /device:TPU:0, one launch (start us, length us, event | category | flops | bytes accessed | tf_op | source)
XLA Modules:
  0.0 348.3 jit_solution(17330387453719186282)
XLA Ops:
  7.2 0.0 reduce-scatter.2.cloned.1.call-start
  7.2 3.5 %copy.12 = f32[8192,4]{1,0:T(8,128)} copy(f32[8192,4]{0,1:T(4,128)} %bitcast.31) | data formatting | bytes 262144 | tf_op jit(solution)/shard_map/transpose | solution.py:15
  10.7 15.9 %mul.23 = f32[8192,4,128]{2,1,0:T(4,128)S(1)} broadcast(f32[8192,4]{1,0:T(8,128)} %copy.12), dimensions={0,1} | broadcast | bytes 16908288 | tf_op jit(solution)/shard_map/mul | solution.py:15
  26.6 11.6 %fusion = bf16[8192,512]{1,0:T(8,128)(2,1)} fusion(f32[1024,8,4,128]{3,2,1,0:T(4,128)S(1)} %bitcast.26, s32[1,8192,512]{2,1,0:T(8,128)} %param.4), kind=kLoop, calls=%fused_computation.1 | loop fusion | flops 12582912 | bytes 41943040 | tf_op jit(solution)/shard_map/convert_element_type | solution.py:29
  38.2 0.0 reduce-scatter.2.cloned.1.call-update
  38.3 89.2 %reduce-scatter.2.cloned.1.call-done = bf16[2048,512]{1,0:T(8,128)(2,1)} async-done(((bf16[8192,512]{1,0:T(8,128)(2,1)}), bf16[2048,512]{1,0:T(8,128)(2,1)}) %reduce-scatter.2.cloned.1.call-update) | async-done | bytes 2097168 | tf_op jit(solution)/shard_map/reduce_scatter | solution.py:28
  127.5 4.6 %all-to-all-start = ((bf16[8,256,512]{2,1,0:T(8,128)(2,1)}), bf16[8,256,512]{2,1,0:T(8,128)(2,1)S(1)}, u32[]{:S(2)}, u32[]{:S(2)}) async-start(bf16[8,256,512]{2,1,0:T(8,128)(2,1)} %bitcast.30), calls=%async_computation.1 | async-start | bytes 4194304 | tf_op jit(solution)/shard_map/all_to_all | solution.py:31
  132.1 0.0 all-gather.2.cloned.1.call-start
  132.1 5.6 %copy.14 = f32[256,4096]{0,1:T(8,128)} copy(f32[256,4096]{1,0:T(8,128)} %param.7) | data formatting | bytes 8388608 | tf_op args[3]
  137.7 5.6 %copy.15 = f32[256,4096]{0,1:T(8,128)} copy(f32[256,4096]{1,0:T(8,128)} %param.6) | data formatting | bytes 8388608 | tf_op args[2]
  143.3 37.8 %all-to-all-done = bf16[8,256,512]{2,1,0:T(8,128)(2,1)S(1)} async-done(((bf16[8,256,512]{2,1,0:T(8,128)(2,1)}), bf16[8,256,512]{2,1,0:T(8,128)(2,1)S(1)}, u32[]{:S(2)}, u32[]{:S(2)}) %all-to-all-start) | async-done | bytes 2097184 | tf_op jit(solution)/shard_map/all_to_all | solution.py:31
  181.1 2.4 copy.13
  183.5 0.0 copy-start
  183.5 2.1 convert_multiply_fusion
  185.6 0.7 copy-done
  186.3 7.3 %fusion.3 = (bf16[256,4096]{0,1:T(8,128)(2,1)}, f32[256,4096]{0,1:T(8,128)}, f32[256,4096]{0,1:T(8,128)}) fusion(f32[256,4096]{0,1:T(8,128)} %copy.15, f32[256,4096]{0,1:T(8,128)S(1)} %copy-done, f32[8,256,512]{1,2,0:T(8,128)S(1)} %convert_multiply_fusion), kind=kLoop, calls=%fused_computation.7 | loop fusion | flops 7340032 | bytes 23068672 | tf_op jit(solution)/shard_map/convert_element_type | solution.py:35
  193.5 52.5 %all_to_all.32 = bf16[256,8,512]{0,2,1:T(8,128)(2,1)S(1)} all-to-all(bf16[256,8,512]{0,2,1:T(8,128)(2,1)} %bitcast.29), channel_id=1, replica_groups=mesh['replica'=4,'fsdp'=8] {'fsdp'}, dimensions={1} | all-to-all | bytes 4194304 | tf_op jit(solution)/shard_map/all_to_all | solution.py:36
  246.1 2.4 copy.16
  248.5 0.0 all-gather.2.cloned.1.call-update
  248.5 5.6 %copy.17 = f32[256,4096]{1,0:T(8,128)} copy(f32[256,4096]{0,1:T(8,128)} %get-tuple-element.7) | data formatting | bytes 8388608
  254.1 6.0 %copy.18 = f32[256,4096]{1,0:T(8,128)} copy(f32[256,4096]{0,1:T(8,128)} %get-tuple-element.8) | data formatting | bytes 8388608
  260.1 74.0 %all-gather.2.cloned.1.call-done = bf16[8192,512]{1,0:T(8,128)(2,1)} async-done(((bf16[2048,512]{1,0:T(8,128)(2,1)}), bf16[8192,512]{1,0:T(8,128)(2,1)}) %all-gather.2.cloned.1.call-update) | async-done | bytes 8388624 | tf_op jit(solution)/shard_map/all_gather | solution.py:37
  334.1 7.3 %copy.22 = bf16[8192,512]{1,0:T(8,128)(2,1)} copy(bf16[8192,512]{1,0:T(8,128)(2,1)} %all-gather.2.cloned.1.call-done) | data formatting | bytes 16777216
Async XLA Ops:
  7.2 120.3 %reduce-scatter.2.cloned.1.call-start = ((), (), s32[]{:S(2)}) async-start(), calls=%async_computation.3 | async-start | bytes 10485760 | tf_op jit(solution)/shard_map/reduce_scatter | solution.py:28
  127.5 53.7 %all-to-all-start = ((bf16[8,256,512]{2,1,0:T(8,128)(2,1)}), bf16[8,256,512]{2,1,0:T(8,128)(2,1)S(1)}, u32[]{:S(2)}, u32[]{:S(2)}) async-start(bf16[8,256,512]{2,1,0:T(8,128)(2,1)} %bitcast.30), calls=%async_computation.1 | async-start | bytes 4194304 | tf_op jit(solution)/shard_map/all_to_all | solution.py:31
  132.1 202.0 %all-gather.2.cloned.1.call-start = ((), (), s32[]{:S(2)}) async-start(), calls=%async_computation.4 | async-start | bytes 10485760 | tf_op jit(solution)/shard_map/all_gather | solution.py:37
  183.5 2.8 copy-start
Sparse Core Ops, SparseCore 0:
  38.4 89.0 reduce-scatter.1
  248.6 85.4 all-gather.1
where the time goes:
time: 349 us; the launch traced here: 348 us
  waiting for transfers between devices  201 us (58%)
  local copies, waits for them, and re-layouts  55 us (16%)
  blocking collectives  52.5 us (15%)
  other arithmetic  21 us (6%)
  between operations  14.1 us (4%)
  starting transfers between devices  4.69 us (1%)
    reduce_scatter x1, waiting for transfers between devices, local(): lax.psum_scatter(delta_local.astype(jnp.bfloat16), 'replica', scatter_dim...  89.2 us
    all_gather x1, waiting for transfers between devices, local(): weights = lax.all_gather(columns, 'replica', axis=0, tiled=True)  74 us
    all_to_all x1, blocking collectives, local(): lax.all_to_all(rounded, 'fsdp', split_axis=1, concat_axis=0, tiled=True)  52.5 us
    all_to_all x1, waiting for transfers between devices, local(): lax.all_to_all(partial_sum.astype(jnp.bfloat16), 'fsdp', split_axis=0, co...  37.8 us
    unnamed x7, local copies, waits for them, and re-layouts  30.8 us
    mul x1, local copies, waits for them, and re-layouts, dequantize(): scaled * jnp.transpose(scales[0])[:, :, None]  15.9 us
    convert_element_type x1, other arithmetic, local(): delta_local.astype(jnp.bfloat16)  11.6 us
    convert_element_type x1, other arithmetic, local(): rounded = new_master.astype(jnp.bfloat16)  7.26 us
  transfers between devices with their start and end apart: 3, of which 3 were waited for; matrix products, arithmetic and copies ran while one was open for 7% of the time, Pallas kernels for 0%

commit v1 on v0

--- a/solution.py
+++ b/solution.py
@@ -28,9 +28,10 @@
     partial_sum = lax.psum_scatter(
         delta_local.astype(jnp.bfloat16), "replica", scatter_dimension=0, tiled=True
     ).astype(jnp.float32)
-    summed = lax.all_to_all(
-        partial_sum.astype(jnp.bfloat16), "fsdp", split_axis=0, concat_axis=1, tiled=True
-    ).astype(partial_sum.dtype)
+    _match_lots_all = lambda xin: jnp.concatenate(
+        lax.all_to_all(jnp.stack(jnp.split(xin, lax.psum(1, "fsdp"), 0), 0), "fsdp", 0, 0), 1
+    )
+    summed = _match_lots_all(partial_sum.astype(jnp.bfloat16)).astype(partial_sum.dtype)
     new_master, new_momentum = outer_update(summed, master, momentum, replica_count)
     rounded = new_master.astype(jnp.bfloat16)
     columns = lax.all_to_all(rounded, "fsdp", split_axis=1, concat_axis=0, tiled=True)

time: 349 us -> 351 us (level)
  blocking collectives: 52.5 us -> 106 us
  waiting for transfers between devices: 201 us -> 175 us
  local copies, waits for them, and re-layouts: 55 us -> 35.1 us
  starting transfers between devices: 4.69 us -> 0.08 us
    all_to_all x0 -> x1, blocking collectives: none -> 53.4 us  [local(): lax.all_to_all(jnp.stack(jnp.split(xin, lax.psum(1, 'fsdp'), 0), 0), 'fsd...]
    all_to_all x1 -> x0, waiting for transfers between devices: 37.8 us -> none  [local(): lax.all_to_all(partial_sum.astype(jnp.bfloat16), 'fsdp', split_axis=0, co...]
    unnamed x7 -> x8, local copies, waits for them, and re-layouts: 30.8 us -> 14.1 us
    all_gather x1, waiting for transfers between devices: 74 us -> 85.6 us  [local(): weights = lax.all_gather(columns, 'replica', axis=0, tiled=True)]
    all_to_all x1 -> x0, starting transfers between devices: 4.62 us -> none  [local(): lax.all_to_all(partial_sum.astype(jnp.bfloat16), 'fsdp', split_axis=0, co...]
  transfers between devices with their start and end apart: 3 -> 2, of which waited for: 3 -> 2; matrix products, arithmetic and copies ran while one was open for 7% -> 0% of each run, Pallas kernels for 0% -> 0%
where the time goes in v1:
time: 351 us
  waiting for transfers between devices  175 us (50%)
  blocking collectives  106 us (30%)
  local copies, waits for them, and re-layouts  35.1 us (10%)
  other arithmetic  21 us (6%)
  between operations  14.1 us (4%)
    reduce_scatter x1, waiting for transfers between devices, local(): lax.psum_scatter(delta_local.astype(jnp.bfloat16), 'replica', scatter_dim...  89.1 us
    all_gather x1, waiting for transfers between devices, local(): weights = lax.all_gather(columns, 'replica', axis=0, tiled=True)  85.6 us
    all_to_all x1, blocking collectives, local(): lax.all_to_all(jnp.stack(jnp.split(xin, lax.psum(1, 'fsdp'), 0), 0), 'fsd...  53.4 us
    all_to_all x1, blocking collectives, local(): lax.all_to_all(rounded, 'fsdp', split_axis=1, concat_axis=0, tiled=True)  52.2 us
    mul x1, local copies, waits for them, and re-layouts, dequantize(): scaled * jnp.transpose(scales[0])[:, :, None]  15.9 us
    unnamed x8, local copies, waits for them, and re-layouts  14.1 us
    convert_element_type x1, other arithmetic, local(): delta_local.astype(jnp.bfloat16)  11.6 us
    convert_element_type x1, other arithmetic, local(): rounded = new_master.astype(jnp.bfloat16)  8.85 us
  transfers between devices with their start and end apart: 2, of which 2 were waited for; matrix products, arithmetic and copies ran while one was open for 0% of the time, Pallas kernels for 0%

profile of v1, /device:TPU:0, one launch (start us, length us, event | category | flops | bytes accessed | tf_op | source)
XLA Modules:
  0.0 350.7 jit_solution(15415753327921154262)
XLA Ops:
  7.2 0.0 reduce-scatter.2.cloned.1.call-start
  7.2 3.5 copy.7
  10.7 15.9 %mul.23 = f32[8192,4,128]{2,1,0:T(4,128)S(1)} broadcast(f32[8192,4]{1,0:T(8,128)} %copy.7), dimensions={0,1} | broadcast | bytes 16908288 | tf_op jit(solution)/shard_map/mul | solution.py:15
  26.6 11.6 %fusion = bf16[8192,512]{1,0:T(8,128)(2,1)} fusion(f32[1024,8,4,128]{3,2,1,0:T(4,128)S(1)} %bitcast.53, s32[1,8192,512]{2,1,0:T(8,128)} %param.4), kind=kLoop, calls=%fused_computation.1 | loop fusion | flops 12582912 | bytes 41943040 | tf_op jit(solution)/shard_map/convert_element_type | solution.py:29
  38.2 0.0 reduce-scatter.2.cloned.1.call-update
  38.3 0.0 all-gather.2.cloned.1.call-start
  38.3 89.1 %reduce-scatter.2.cloned.1.call-done = bf16[2048,512]{1,0:T(8,128)(2,1)} async-done(((bf16[8192,512]{1,0:T(8,128)(2,1)}), bf16[2048,512]{1,0:T(8,128)(2,1)}) %reduce-scatter.2.cloned.1.call-update) | async-done | bytes 2097168 | tf_op jit(solution)/shard_map/reduce_scatter | solution.py:28
  127.5 1.0 fusion.8
  128.4 1.0 fusion.7
  129.4 1.0 fusion.6
  130.4 1.0 fusion.5
  131.3 1.0 fusion.4
  132.3 1.0 fusion.3
  133.3 1.0 fusion.2
  134.3 1.0 fusion.1
  135.2 53.4 %all_to_all.24 = bf16[8,256,512]{2,1,0:T(8,128)(2,1)S(1)} all-to-all(bf16[8,256,512]{2,1,0:T(8,128)(2,1)S(1)} %fusion.1), channel_id=1, replica_groups=mesh['replica'=4,'fsdp'=8] {'fsdp'}, dimensions={0} | all-to-all | bytes 4194304 | tf_op jit(solution)/shard_map/all_to_all | solution.py:32
  188.7 0.6 multiply_bitcast_fusion
  189.3 0.5 copy.11
  189.7 8.8 %fusion.9 = (bf16[256,4096]{1,0:T(8,128)(2,1)S(1)}, f32[256,4096]{1,0:T(8,128)}, f32[256,4096]{1,0:T(8,128)}) fusion(f32[256,4096]{1,0:T(8,128)} %param.6, f32[256,4096]{1,0:T(8,128)S(1)} %bitcast.54, f32[256,4096]{1,0:T(8,128)} %param.7), kind=kLoop, calls=%fused_computation.22 | loop fusion | flops 7340032 | bytes 23068672 | tf_op jit(solution)/shard_map/convert_element_type | solution.py:36
  198.6 0.2 copy.15
  198.8 52.2 %all_to_all.25 = bf16[256,8,512]{2,0,1:T(8,128)(2,1)} all-to-all(bf16[256,8,512]{2,0,1:T(8,128)(2,1)S(1)} %bitcast.56), channel_id=1, replica_groups=mesh['replica'=4,'fsdp'=8] {'fsdp'}, dimensions={1} | all-to-all | bytes 4194304 | tf_op jit(solution)/shard_map/all_to_all | solution.py:37
  251.0 0.0 all-gather.2.cloned.1.call-update
  251.0 85.6 %all-gather.2.cloned.1.call-done = bf16[8192,512]{1,0:T(8,128)(2,1)} async-done(((bf16[2048,512]{1,0:T(8,128)(2,1)}), bf16[8192,512]{1,0:T(8,128)(2,1)}) %all-gather.2.cloned.1.call-update) | async-done | bytes 8388624 | tf_op jit(solution)/shard_map/all_gather | solution.py:38
  336.6 7.3 %copy.24 = bf16[8192,512]{1,0:T(8,128)(2,1)} copy(bf16[8192,512]{1,0:T(8,128)(2,1)} %all-gather.2.cloned.1.call-done) | data formatting | bytes 16777216
Async XLA Ops:
  7.2 120.3 %reduce-scatter.2.cloned.1.call-start = ((), (), s32[]{:S(2)}) async-start(), calls=%async_computation.3 | async-start | bytes 10485760 | tf_op jit(solution)/shard_map/reduce_scatter | solution.py:28
  38.3 298.3 %all-gather.2.cloned.1.call-start = ((), (), s32[]{:S(2)}) async-start(), calls=%async_computation.4 | async-start | bytes 10485760 | tf_op jit(solution)/shard_map/all_gather | solution.py:38
Sparse Core Ops, SparseCore 0:
  38.4 89.0 reduce-scatter.1
  251.1 85.4 all-gather.1
